TPU v7x, 32 devices: a whole 2x2x4 slice. The times are simulated.
32 devices in a mesh: samp: 4 (over y, x), snp: 8 (over z, core).
Axes of the slice: x: 2, y: 2, z: 4, core: 2. Of those that a mesh axis runs over, the one named last changes fastest.
Arguments:
- genotypes: int32 [8192, 8192], P('samp', 'snp'), may hold values from 0 to 2
- win_lo: int32 [8192], P('snp'), may hold values from 0 to 8191, as said below
- win_hi: int32 [8192], P('snp'), may hold values from 0 to 8191, as said below
- annotation: int32 [8192], P('snp'), may hold values from 0 to 127
- chromosome: int32 [8192], P('snp'), may hold values from 0 to 21, never falling along the last dimension, each value on 1 to 512 neighbouring positions
- chi_square: float32 [8192], P('snp'), may hold values from 0.3 to 60
Outputs:
- annotation_scores: float32 [128, 8192], P('snp')
- gram: float32 [128, 128], replicated
- moments: float32 [2, 128], replicated
- totals: float32 [2], replicated
Inputs may be any that keep to these rules, and one draw needn't show every extreme that they name: i - 512 <= win_lo[i] <= i, nondecreasing in i; the distance 512 is reached. i <= win_hi[i] <= i + 512, nondecreasing in i; the distance 512 is reached.
All inputs are finite; a program needn't handle non-finite values.
Results may differ from a plain program's by a relative error of at most 0.0003.
The roundings to bfloat16 on the way count: a program that leaves them out, or rounds other values in their place, can miss the bound.
Values may be sent and summed in bfloat16 or wider, within the bound.
A program may use at most 64 MiB of HBM per device.

v0:
```python
import jax
import jax.numpy as jnp
from jax import lax
from jax.sharding import PartitionSpec as P

A = 128


def extended(cells, sides, width):
    for axis, dim in sides:
        count = lax.axis_size(axis)
        ends = count - 1
        head = lax.slice_in_dim(cells, 0, width, axis=dim)
        tail = lax.slice_in_dim(cells, cells.shape[dim] - width, cells.shape[dim], axis=dim)
        cells = jnp.concatenate(
            [
                lax.ppermute(tail, axis, [(i, (i + 1) % count) for i in range(ends)]),
                cells,
                lax.ppermute(head, axis, [((i + 1) % count, i) for i in range(ends)]),
            ],
            axis=dim,
        )
    return cells


def body(genotypes, win_lo, win_hi, annotation, chromosome, chi_square):
    samp_rows, block_cols = genotypes.shape
    reach = block_cols // 2
    samp_count = lax.axis_size("samp")
    total_samples = samp_rows * samp_count
    dosage = genotypes.astype(jnp.float32)
    dose_sums, dose_squares = lax.psum((jnp.sum(dosage, 0), jnp.sum(dosage * dosage, 0)), "samp")
    mean_dose = dose_sums / total_samples
    variance = dose_squares / total_samples - mean_dose * mean_dose
    standard = ((dosage - mean_dose) * lax.rsqrt(variance + 1e-05)).astype(jnp.bfloat16)
    first_snp = lax.axis_index("snp") * block_cols
    labels = jnp.arange(A, dtype=jnp.int32)
    own_labels = jnp.stack([annotation, chromosome]).astype(jnp.bfloat16)
    wide_z, wide_labels = (
        extended(standard, (("snp", 1),), reach),
        extended(own_labels, (("snp", 1),), reach),
    )
    annot_wide = wide_labels[0].astype(jnp.int32)
    chrom_wide = wide_labels[1].astype(jnp.int32)
    span = wide_z.shape[1] - block_cols + reach

    def tile_piece(row_start, count):
        band = row_start // reach * reach
        rows_z = lax.dynamic_slice_in_dim(standard, row_start, count, 1)
        cols_z = lax.dynamic_slice_in_dim(wide_z, band, span, 1)
        return lax.dot_general(
            rows_z, cols_z, (((0,), (0,)), ((), ())), preferred_element_type=jnp.float32
        )

    share = block_cols // samp_count
    row_start = jnp.int32(0)
    tile = lax.psum_scatter(
        jnp.concatenate(
            [
                tile_piece(row_start + offset * share, share)
                for offset in range(share * lax.axis_size("samp") // share)
            ],
            0,
        ),
        "samp",
        scatter_dimension=0,
        tiled=True,
    )
    row_begin = lax.axis_index("samp") * share
    row_start = row_begin + 0
    band = row_start // reach * reach
    corr = tile / total_samples
    square = corr * corr
    adjusted = square - (1.0 - square) / (total_samples - 2)
    col_ids = first_snp + band - reach + jnp.arange(span, dtype=jnp.int32)
    lower_end = lax.dynamic_slice_in_dim(win_lo, row_start, share)
    upper_end = lax.dynamic_slice_in_dim(win_hi, row_start, share)
    chrom_rows = lax.dynamic_slice_in_dim(chromosome, row_start, share)
    chrom_cols = lax.dynamic_slice_in_dim(chrom_wide, band, span)
    annot_cols = lax.dynamic_slice_in_dim(annot_wide, band, span)
    inside = (col_ids[None, :] >= lower_end[:, None]) & (col_ids[None, :] <= upper_end[:, None])
    inside = inside & (chrom_cols[None, :] == chrom_rows[:, None])
    kept = jnp.where(inside, adjusted, 0.0)
    member = (annot_cols[:, None] == labels[None, :]).astype(jnp.float32)
    part_scores = lax.dot_general(
        member,
        kept,
        (((0,), (1,)), ((), ())),
        precision=lax.Precision.HIGHEST,
        preferred_element_type=jnp.float32,
    )
    scores = lax.all_gather(part_scores, "samp", axis=1, tiled=True)
    weights = 1.0 / jnp.sum(scores, 0)
    weighted = scores * weights[None, :]
    gram_part = lax.dot_general(
        weighted,
        scores,
        (((1,), (1,)), ((), ())),
        precision=lax.Precision.HIGHEST,
        preferred_element_type=jnp.float32,
    )
    moment_part = jnp.stack([jnp.sum(weighted, 1), jnp.sum(weighted * chi_square[None, :], 1)])
    total_part = jnp.stack([jnp.sum(weights), jnp.sum(weights * chi_square)])
    gram, moments, totals = lax.psum((gram_part, moment_part, total_part), "snp")
    snp_total = block_cols * lax.axis_size("snp")
    scale = A / snp_total
    regrouped = lax.all_to_all(scores, "snp", split_axis=0, concat_axis=1, tiled=True)
    return (regrouped, scale * gram, scale * moments, totals / snp_total)


def solution(mesh):
    in_specs = (P("samp", "snp"), P("snp"), P("snp"), P("snp"), P("snp"), P("snp"))
    out_specs = (P("snp", None), P(), P(), P())
    return jax.shard_map(body, mesh=mesh, in_specs=in_specs, out_specs=out_specs, check_vma=False)
```

profile of v0, /device:TPU:0, one launch (start us, length us, event | category | flops | bytes accessed | tf_op | source)
XLA Modules:
  0.0 220.2 jit_solution(12471998760176331040)
XLA Ops:
  7.2 0.0 reduce-scatter.2.cloned.1.call-start
  7.2 4.5 %convert_reduce_fusion = (f32[1024]{0:T(1024)S(1)}, f32[1024]{0:T(1024)S(1)}) fusion(s32[2048,1024]{1,0:T(8,128)} %param.6), kind=kLoop, calls=%fused_computation.2 | loop fusion | flops 8386560 | bytes 8396800 | tf_op jit(solution)/shard_map/reduce_sum | solution.py:32
  11.7 11.5 %all-reduce.1 = (f32[1024]{0:T(1024)S(1)}, f32[1024]{0:T(1024)S(1)}) all-reduce(f32[1024]{0:T(1024)S(1)} %get-tuple-element.5, f32[1024]{0:T(1024)S(1)} %get-tuple-element.4), channel_id=1, replica_groups=mesh['samp'=4,'snp'=8] {'samp'}, use_global_device_ids=true, to_apply=%region_3.0 | all-reduce | flops 2048 | bytes 16384 | tf_op jit(solution)/shard_map/psum | solution.py:32
  23.3 4.7 %multiply_convert_fusion = bf16[2048,1024]{1,0:T(8,128)(2,1)S(1)} fusion(s32[2048,1024]{1,0:T(8,128)} %param.6, f32[1024]{0:T(1024)S(1)} %get-tuple-element.22, f32[1024]{0:T(1024)S(1)} %get-tuple-element.21), kind=kLoop, calls=%fused_computation | loop fusion | flops 8388608 | bytes 12591104 | tf_op jit(solution)/shard_map/convert_element_type | solution.py:35
  28.0 0.3 fusion.48
  28.3 1.4 collective-permute-start.2
  29.8 1.3 collective-permute-start.3
  31.1 2.3 %collective-permute-done.2 = bf16[2048,512]{1,0:T(8,128)(2,1)S(1)} collective-permute-done((bf16[2048,512]{1,0:T(8,128)(2,1)S(1)}, bf16[2048,512]{1,0:T(8,128)(2,1)S(1)}, u32[]{:S(2)}, u32[]{:S(2)}) %collective-permute-start.2) | collective-permute-done | bytes 2097184 | tf_op jit(solution)/shard_map/ppermute | solution.py:17
  33.4 1.8 fusion.2
  35.2 1.8 fusion.3
  37.0 0.4 collective-permute-done.3
  37.5 1.8 fusion.1
  39.3 1.8 fusion
  41.1 2.9 %pad_maximum_fusion.2 = f32[1024,1536]{1,0:T(8,128)} fusion(f32[256,1536]{1,0:T(8,128)S(1)} %fusion, f32[256,1536]{1,0:T(8,128)S(1)} %fusion.1, f32[256,1536]{1,0:T(8,128)S(1)} %fusion.2, f32[256,1536]{1,0:T(8,128)S(1)} %fusion.3), kind=kLoop, calls=%fused_computation.5 | loop fusion | flops 4718592 | bytes 12582912 | tf_op jit(solution)/shard_map/concatenate | solution.py:58
  44.0 0.0 copy-start.2
  44.0 0.0 copy-start.1
  44.0 0.0 reduce-scatter.2.cloned.1.call-update
  44.1 0.0 copy-start
  44.1 0.0 all-reduce.4.cloned.1.call-start
  44.1 0.6 copy-done.2
  44.7 0.0 copy-done.1
  44.8 23.7 %collective-permute-start = (bf16[2,512]{1,0:T(2,128)(2,1)S(1)}, bf16[2,512]{1,0:T(2,128)(2,1)S(1)}, u32[]{:S(2)}, u32[]{:S(2)}) collective-permute-start(bf16[2,512]{1,0:T(2,128)(2,1)S(1)} %get-tuple-element.18), channel_id=1, source_target_pairs={{0,1},{1,2},{2,3},{3,4},{4,5},{5,6},{6,7},{8,9},{9,10},{10,11},{11... | collective-permute-start | bytes 6152 | tf_op jit(solution)/shard_map/ppermute | solution.py:17
  68.5 1.3 collective-permute-start.1
  69.8 0.1 dynamic_slice.41
  69.9 0.8 dynamic_slice.37
  70.7 0.8 dynamic_slice.38
  71.4 0.0 collective-permute-done
  71.4 1.4 collective-permute-done.1
  72.9 62.5 %reduce-scatter.2.cloned.1.call-done = f32[256,1536]{1,0:T(8,128)} async-done(((f32[1024,1536]{1,0:T(8,128)}), f32[256,1536]{1,0:T(8,128)}) %reduce-scatter.2.cloned.1.call-update) | async-done | bytes 1572880 | tf_op jit(solution)/shard_map/reduce_scatter | solution.py:57
  135.5 3.0 %fusion.4 = f32[128,256]{1,0:T(8,128)S(1)} fusion(f32[256,1536]{1,0:T(8,128)} %reduce-scatter.2.cloned.1.call-done, s32[1536]{0:T(1024)S(1)} %get-tuple-element.23, s32[1536]{0:T(1024)S(1)} %iota_add_fusion, s32[256]{0:T(256)S(1)} %dynamic_slice.41, s32[256]{0:T(256)S(1)} %dynamic_slice.38, s32[256]{0:T(256)S(1)} %dynamic_slice.37, ...), kind=kOutput, calls=%fused_computation.10 | convolution fusion | flops 608698368 | bytes 1725440 | tf_op jit(solution)/shard_map/dot_general | solution.py:85
  138.5 10.6 %all_gather.3 = f32[128,1024]{1,0:T(8,128)} all-gather(f32[128,256]{1,0:T(8,128)S(1)} %fusion.4), channel_id=1, replica_groups=mesh['samp'=4,'snp'=8] {'samp'}, dimensions={1}, use_global_device_ids=true | all-gather | bytes 655360 | tf_op jit(solution)/shard_map/all_gather | solution.py:92
  149.1 1.1 reduce_sum.65
  150.2 0.0 copy-done
  150.2 0.6 fusion.47
  150.8 2.4 %fusion.30 = f32[128,128]{1,0:T(8,128)} fusion(f32[128,1024]{1,0:T(8,128)} %all_gather.3, f32[1024]{0:T(1024)S(1)} %get-tuple-element.20), kind=kOutput, calls=%fused_computation.39 | convolution fusion | flops 201457664 | bytes 593920 | tf_op jit(solution)/shard_map/dot_general | solution.py:95
  153.3 0.0 all-reduce.4.cloned.1.call-update
  153.3 4.6 %all-to-all-start = ((f32[8,16,1024]{2,1,0:T(8,128)}), f32[8,16,1024]{2,1,0:T(8,128)S(1)}, u32[]{:S(2)}, u32[]{:S(2)}) async-start(f32[8,16,1024]{2,1,0:T(8,128)} %bitcast), calls=%async_computation.1 | async-start | bytes 1048576 | tf_op jit(solution)/shard_map/all_to_all | solution.py:107
  157.9 1.4 pad_maximum_fusion.10
  159.3 1.2 multiply_reduce_fusion.1
  160.5 18.6 %all-reduce = (f32[2,128]{1,0:T(2,128)S(1)}, f32[2]{0:T(128)S(1)}) all-reduce(f32[2,128]{1,0:T(2,128)S(1)} %pad_maximum_fusion.9, f32[2]{0:T(128)S(1)} %pad_maximum_fusion.10), channel_id=1, replica_groups=mesh['samp'=4,'snp'=8] {'snp'}, use_global_device_ids=true, to_apply=%region_9.10 | all-reduce | flops 258 | bytes 2064 | tf_op jit(solution)/shard_map/psum | solution.py:104
  179.0 0.6 broadcast_multiply_fusion.2
  179.6 0.5 broadcast_multiply_fusion.3
  180.1 30.9 %all-reduce.4.cloned.1.call-done = f32[128,128]{1,0:T(8,128)} async-done(((f32[128,128]{1,0:T(8,128)}), f32[128,128]{1,0:T(8,128)}) %all-reduce.4.cloned.1.call-update) | async-done | bytes 65552 | tf_op jit(solution)/shard_map/psum | solution.py:104
  211.1 1.5 broadcast_multiply_fusion
  212.5 0.0 all-to-all-done
  212.5 0.8 copy.11
  (11 shorter events, 0.1 us)
Async XLA Ops:
  7.2 128.3 %reduce-scatter.2.cloned.1.call-start = ((), (), s32[]{:S(2)}) async-start(), calls=%async_computation.2 | async-start | bytes 7864320 | tf_op jit(solution)/shard_map/reduce_scatter | solution.py:57
  28.3 5.1 %collective-permute-start.2 = (bf16[2048,512]{1,0:T(8,128)(2,1)S(1)}, bf16[2048,512]{1,0:T(8,128)(2,1)S(1)}, u32[]{:S(2)}, u32[]{:S(2)}) collective-permute-start(bf16[2048,512]{1,0:T(8,128)(2,1)S(1)} %get-tuple-element.14), channel_id=1, source_target_pairs={{0,1},{1,2},{2,3},{3,4},{4,5},{5,6},{6,7},{8,9},{9,10},{10,11},{11... | collective-permute-start | bytes 6291464 | tf_op jit(solution)/shard_map/ppermute | solution.py:17
  29.8 7.7 %collective-permute-start.3 = (bf16[2048,512]{1,0:T(8,128)(2,1)S(1)}, bf16[2048,512]{1,0:T(8,128)(2,1)S(1)}, u32[]{:S(2)}, u32[]{:S(2)}) collective-permute-start(bf16[2048,512]{1,0:T(8,128)(2,1)S(1)} %get-tuple-element.15), channel_id=1, source_target_pairs={{1,0},{2,1},{3,2},{4,3},{5,4},{6,5},{7,6},{9,8},{10,9},{11,10},{12... | collective-permute-start | bytes 6291464 | tf_op jit(solution)/shard_map/ppermute | solution.py:19
  44.0 0.7 copy-start.2
  44.0 0.7 copy-start.1
  44.1 106.2 %copy-start = (f32[1024]{0:T(1024)S(1)}, f32[1024]{0:T(1024)}, u32[]{:S(2)}) copy-start(f32[1024]{0:T(1024)} %param.11) | copy-start | bytes 12292
  44.1 167.0 %all-reduce.4.cloned.1.call-start = ((), (), s32[]{:S(2)}) async-start(), calls=%async_computation.3 | async-start | bytes 131072 | tf_op jit(solution)/shard_map/psum | solution.py:104
  44.8 26.6 %collective-permute-start = (bf16[2,512]{1,0:T(2,128)(2,1)S(1)}, bf16[2,512]{1,0:T(2,128)(2,1)S(1)}, u32[]{:S(2)}, u32[]{:S(2)}) collective-permute-start(bf16[2,512]{1,0:T(2,128)(2,1)S(1)} %get-tuple-element.18), channel_id=1, source_target_pairs={{0,1},{1,2},{2,3},{3,4},{4,5},{5,6},{6,7},{8,9},{9,10},{10,11},{11... | collective-permute-start | bytes 6152 | tf_op jit(solution)/shard_map/ppermute | solution.py:17
  68.5 4.3 %collective-permute-start.1 = (bf16[2,512]{1,0:T(2,128)(2,1)S(1)}, bf16[2,512]{1,0:T(2,128)(2,1)S(1)}, u32[]{:S(2)}, u32[]{:S(2)}) collective-permute-start(bf16[2,512]{1,0:T(2,128)(2,1)S(1)} %get-tuple-element.19), channel_id=1, source_target_pairs={{1,0},{2,1},{3,2},{4,3},{5,4},{6,5},{7,6},{9,8},{10,9},{11,10},{12... | collective-permute-start | bytes 6152 | tf_op jit(solution)/shard_map/ppermute | solution.py:19
  153.3 59.3 %all-to-all-start = ((f32[8,16,1024]{2,1,0:T(8,128)}), f32[8,16,1024]{2,1,0:T(8,128)S(1)}, u32[]{:S(2)}, u32[]{:S(2)}) async-start(f32[8,16,1024]{2,1,0:T(8,128)} %bitcast), calls=%async_computation.1 | async-start | bytes 1048576 | tf_op jit(solution)/shard_map/all_to_all | solution.py:107
Sparse Core Ops, SparseCore 0:
  44.2 91.2 reduce-scatter.1
  153.4 57.6 all-reduce.3
where the time goes:
time: 221 us; the launch traced here: 220 us
  waiting for transfers between devices  97.7 us (44%)
  blocking collectives  40.8 us (18%)
  starting transfers between devices  32.4 us (15%)
  other arithmetic  19 us (9%)
  between operations  14.2 us (6%)
  matrix products  12.7 us (6%)
  local copies, waits for them, and re-layouts  3.39 us (2%)
    reduce_scatter x1, waiting for transfers between devices, body(): lax.psum_scatter(jnp.concatenate([tile_piece(row_start + offset * share,...  62.5 us
    psum x1, waiting for transfers between devices, body(): lax.psum((gram_part, moment_part, total_part), 'snp')  30.9 us
    ppermute x2, starting transfers between devices, extended(): lax.ppermute(tail, axis, [(i, (i + 1) % count) for i in range(ends)])  25.1 us
    psum x1, blocking collectives, body(): lax.psum((gram_part, moment_part, total_part), 'snp')  18.6 us
    psum x1, blocking collectives, body(): lax.psum((jnp.sum(dosage, 0), jnp.sum(dosage * dosage, 0)), 'samp')  11.5 us
    all_gather x1, blocking collectives, body(): scores = lax.all_gather(part_scores, 'samp', axis=1, tiled=True)  10.6 us
    dot_general x4, matrix products, tile_piece(): lax.dot_general(rows_z, cols_z, (((0,), (0,)), ((), ())), preferred_eleme...  7.27 us
    convert_element_type x1, other arithmetic, body(): ((dosage - mean_dose) * lax.rsqrt(variance + 1e-05)).astype(jnp.bfloat16)  4.68 us
  transfers between devices with their start and end apart: 7, of which 5 were waited for; matrix products, arithmetic and copies ran while one was open for 5% of the time, Pallas kernels for 0%

commit v1 on v0

--- a/solution.py
+++ b/solution.py
@@ -104,7 +104,10 @@
     gram, moments, totals = lax.psum((gram_part, moment_part, total_part), "snp")
     snp_total = block_cols * lax.axis_size("snp")
     scale = A / snp_total
-    regrouped = lax.all_to_all(scores, "snp", split_axis=0, concat_axis=1, tiled=True)
+    regrouped = jnp.concatenate(
+        lax.all_to_all(jnp.stack(jnp.split(scores, lax.axis_size("snp"), axis=0)), "snp", 0, 0),
+        axis=1,
+    )
     return (regrouped, scale * gram, scale * moments, totals / snp_total)
 
 

time: 221 us -> 218 us (0.986)
  waiting for transfers between devices: 97.7 us -> 92.3 us
  local copies, waits for them, and re-layouts: 3.39 us -> 8.47 us
    psum x1, waiting for transfers between devices: 30.9 us -> 25.6 us  [body(): lax.psum((gram_part, moment_part, total_part), 'snp')]
    unnamed x6 -> x13, local copies, waits for them, and re-layouts: 0.61 us -> 5.05 us
  transfers between devices with their start and end apart: 7 -> 7, of which waited for: 5 -> 5; matrix products, arithmetic and copies ran while one was open for 5% -> 6% of each run, Pallas kernels for 0% -> 0%
where the time goes in v1:
time: 218 us; the launch traced here: 217 us
  waiting for transfers between devices  92.3 us (42%)
  blocking collectives  41.3 us (19%)
  starting transfers between devices  32.3 us (15%)
  other arithmetic  16.9 us (8%)
  between operations  14.2 us (7%)
  matrix products  11.5 us (5%)
  local copies, waits for them, and re-layouts  8.47 us (4%)
    reduce_scatter x1, waiting for transfers between devices, body(): lax.psum_scatter(jnp.concatenate([tile_piece(row_start + offset * share,...  62.5 us
    psum x1, waiting for transfers between devices, body(): lax.psum((gram_part, moment_part, total_part), 'snp')  25.6 us
    ppermute x2, starting transfers between devices, extended(): lax.ppermute(tail, axis, [(i, (i + 1) % count) for i in range(ends)])  25.1 us
    psum x1, blocking collectives, body(): lax.psum((gram_part, moment_part, total_part), 'snp')  19.6 us
    psum x1, blocking collectives, body(): lax.psum((jnp.sum(dosage, 0), jnp.sum(dosage * dosage, 0)), 'samp')  11.5 us
    all_gather x1, blocking collectives, body(): scores = lax.all_gather(part_scores, 'samp', axis=1, tiled=True)  10.1 us
    dot_general x4, matrix products, tile_piece(): lax.dot_general(rows_z, cols_z, (((0,), (0,)), ((), ())), preferred_eleme...  7.27 us
    unnamed x13, local copies, waits for them, and re-layouts  5.05 us
  transfers between devices with their start and end apart: 7, of which 5 were waited for; matrix products, arithmetic and copies ran while one was open for 6% of the time, Pallas kernels for 0%

profile of v1, /device:TPU:0, one launch (start us, length us, event | category | flops | bytes accessed | tf_op | source)
XLA Modules:
  0.0 217.1 jit_solution(8970355465411531668)
XLA Ops:
  7.2 0.0 reduce-scatter.2.cloned.1.call-start
  7.2 4.5 %convert_reduce_fusion = (f32[1024]{0:T(1024)S(1)}, f32[1024]{0:T(1024)S(1)}) fusion(s32[2048,1024]{1,0:T(8,128)} %param.6), kind=kLoop, calls=%fused_computation.2 | loop fusion | flops 8386560 | bytes 8396800 | tf_op jit(solution)/shard_map/reduce_sum | solution.py:32
  11.7 11.5 %all-reduce.1 = (f32[1024]{0:T(1024)S(1)}, f32[1024]{0:T(1024)S(1)}) all-reduce(f32[1024]{0:T(1024)S(1)} %get-tuple-element.5, f32[1024]{0:T(1024)S(1)} %get-tuple-element.4), channel_id=1, replica_groups=mesh['samp'=4,'snp'=8] {'samp'}, use_global_device_ids=true, to_apply=%region_3.0 | all-reduce | flops 2048 | bytes 16384 | tf_op jit(solution)/shard_map/psum | solution.py:32
  23.3 4.7 %multiply_convert_fusion = bf16[2048,1024]{1,0:T(8,128)(2,1)S(1)} fusion(s32[2048,1024]{1,0:T(8,128)} %param.6, f32[1024]{0:T(1024)S(1)} %get-tuple-element.22, f32[1024]{0:T(1024)S(1)} %get-tuple-element.21), kind=kLoop, calls=%fused_computation | loop fusion | flops 8388608 | bytes 12591104 | tf_op jit(solution)/shard_map/convert_element_type | solution.py:35
  28.0 0.3 fusion.56
  28.3 1.4 collective-permute-start.2
  29.8 1.3 collective-permute-start.3
  31.1 2.3 %collective-permute-done.2 = bf16[2048,512]{1,0:T(8,128)(2,1)S(1)} collective-permute-done((bf16[2048,512]{1,0:T(8,128)(2,1)S(1)}, bf16[2048,512]{1,0:T(8,128)(2,1)S(1)}, u32[]{:S(2)}, u32[]{:S(2)}) %collective-permute-start.2) | collective-permute-done | bytes 2097184 | tf_op jit(solution)/shard_map/ppermute | solution.py:17
  33.4 1.8 fusion.2
  35.2 1.8 fusion.3
  37.0 0.4 collective-permute-done.3
  37.5 1.8 fusion.1
  39.3 1.8 fusion
  41.1 2.9 %pad_maximum_fusion.2 = f32[1024,1536]{1,0:T(8,128)} fusion(f32[256,1536]{1,0:T(8,128)S(1)} %fusion, f32[256,1536]{1,0:T(8,128)S(1)} %fusion.1, f32[256,1536]{1,0:T(8,128)S(1)} %fusion.2, f32[256,1536]{1,0:T(8,128)S(1)} %fusion.3), kind=kLoop, calls=%fused_computation.5 | loop fusion | flops 4718592 | bytes 12582912 | tf_op jit(solution)/shard_map/concatenate | solution.py:58
  44.0 0.0 reduce-scatter.2.cloned.1.call-update
  44.1 0.0 copy-start
  44.1 0.0 all-reduce.4.cloned.1.call-start
  44.1 0.6 copy-done.2
  44.8 23.7 %collective-permute-start = (bf16[2,512]{1,0:T(2,128)(2,1)S(1)}, bf16[2,512]{1,0:T(2,128)(2,1)S(1)}, u32[]{:S(2)}, u32[]{:S(2)}) collective-permute-start(bf16[2,512]{1,0:T(2,128)(2,1)S(1)} %get-tuple-element.18), channel_id=1, source_target_pairs={{0,1},{1,2},{2,3},{3,4},{4,5},{5,6},{6,7},{8,9},{9,10},{10,11},{11... | collective-permute-start | bytes 6152 | tf_op jit(solution)/shard_map/ppermute | solution.py:17
  68.5 1.3 collective-permute-start.1
  69.8 0.1 dynamic_slice.41
  69.9 0.8 dynamic_slice.37
  70.7 0.8 dynamic_slice.38
  71.4 0.0 collective-permute-done
  71.4 1.4 collective-permute-done.1
  72.9 62.5 %reduce-scatter.2.cloned.1.call-done = f32[256,1536]{1,0:T(8,128)} async-done(((f32[1024,1536]{1,0:T(8,128)}), f32[256,1536]{1,0:T(8,128)}) %reduce-scatter.2.cloned.1.call-update) | async-done | bytes 1572880 | tf_op jit(solution)/shard_map/reduce_scatter | solution.py:57
  135.5 3.0 %fusion.4 = f32[128,256]{1,0:T(8,128)S(1)} fusion(f32[256,1536]{1,0:T(8,128)} %reduce-scatter.2.cloned.1.call-done, s32[1536]{0:T(1024)S(1)} %get-tuple-element.23, s32[1536]{0:T(1024)S(1)} %iota_add_fusion, s32[256]{0:T(256)S(1)} %dynamic_slice.41, s32[256]{0:T(256)S(1)} %dynamic_slice.38, s32[256]{0:T(256)S(1)} %dynamic_slice.37, ...), kind=kOutput, calls=%fused_computation.10 | convolution fusion | flops 608698368 | bytes 1725440 | tf_op jit(solution)/shard_map/dot_general | solution.py:85
  138.5 10.1 %all_gather.3 = f32[128,1024]{1,0:T(8,128)S(1)} all-gather(f32[128,256]{1,0:T(8,128)S(1)} %fusion.4), channel_id=1, replica_groups=mesh['samp'=4,'snp'=8] {'samp'}, dimensions={1}, use_global_device_ids=true | all-gather | bytes 655360 | tf_op jit(solution)/shard_map/all_gather | solution.py:92
  148.6 0.6 fusion.43
  149.3 0.6 fusion.55
  149.9 1.2 fusion.30
  151.1 0.0 all-reduce.4.cloned.1.call-update
  151.1 0.6 fusion.42
  151.8 0.6 fusion.41
  152.4 0.6 fusion.40
  153.0 0.6 fusion.39
  153.7 0.6 fusion.38
  154.3 0.6 fusion.37
  154.9 0.6 fusion.36
  155.6 4.6 %all-to-all-start = ((f32[8,16,1024]{2,1,0:T(8,128)}), f32[8,16,1024]{2,1,0:T(8,128)S(1)}, u32[]{:S(2)}, u32[]{:S(2)}) async-start(f32[8,16,1024]{2,1,0:T(8,128)} %fusion.36), calls=%async_computation.1 | async-start | bytes 1048576 | tf_op jit(solution)/shard_map/all_to_all | solution.py:108
  160.1 1.4 pad_maximum_fusion.10
  161.5 0.2 multiply_reduce_fusion.1
  161.7 19.6 %all-reduce = (f32[2,128]{1,0:T(2,128)S(1)}, f32[2]{0:T(128)S(1)}) all-reduce(f32[2,128]{1,0:T(2,128)S(1)} %pad_maximum_fusion.9, f32[2]{0:T(128)S(1)} %pad_maximum_fusion.10), channel_id=1, replica_groups=mesh['samp'=4,'snp'=8] {'snp'}, use_global_device_ids=true, to_apply=%region_9.10 | all-reduce | flops 258 | bytes 2064 | tf_op jit(solution)/shard_map/psum | solution.py:104
  181.3 0.6 broadcast_multiply_fusion.2
  181.9 0.5 broadcast_multiply_fusion.3
  182.4 25.6 %all-reduce.4.cloned.1.call-done = f32[128,128]{1,0:T(8,128)} async-done(((f32[128,128]{1,0:T(8,128)}), f32[128,128]{1,0:T(8,128)}) %all-reduce.4.cloned.1.call-update) | async-done | bytes 65552 | tf_op jit(solution)/shard_map/psum | solution.py:104
  208.0 1.5 broadcast_multiply_fusion
  209.5 0.8 copy.11
  (17 shorter events, 0.2 us)
Async XLA Ops:
  7.2 128.3 %reduce-scatter.2.cloned.1.call-start = ((), (), s32[]{:S(2)}) async-start(), calls=%async_computation.2 | async-start | bytes 7864320 | tf_op jit(solution)/shard_map/reduce_scatter | solution.py:57
  28.3 5.1 %collective-permute-start.2 = (bf16[2048,512]{1,0:T(8,128)(2,1)S(1)}, bf16[2048,512]{1,0:T(8,128)(2,1)S(1)}, u32[]{:S(2)}, u32[]{:S(2)}) collective-permute-start(bf16[2048,512]{1,0:T(8,128)(2,1)S(1)} %get-tuple-element.14), channel_id=1, source_target_pairs={{0,1},{1,2},{2,3},{3,4},{4,5},{5,6},{6,7},{8,9},{9,10},{10,11},{11... | collective-permute-start | bytes 6291464 | tf_op jit(solution)/shard_map/ppermute | solution.py:17
  29.8 7.7 %collective-permute-start.3 = (bf16[2048,512]{1,0:T(8,128)(2,1)S(1)}, bf16[2048,512]{1,0:T(8,128)(2,1)S(1)}, u32[]{:S(2)}, u32[]{:S(2)}) collective-permute-start(bf16[2048,512]{1,0:T(8,128)(2,1)S(1)} %get-tuple-element.15), channel_id=1, source_target_pairs={{1,0},{2,1},{3,2},{4,3},{5,4},{6,5},{7,6},{9,8},{10,9},{11,10},{12... | collective-permute-start | bytes 6291464 | tf_op jit(solution)/shard_map/ppermute | solution.py:19
  44.0 0.7 copy-start.2
  44.0 0.7 copy-start.1
  44.1 105.2 %copy-start = (f32[1024]{0:T(1024)S(1)}, f32[1024]{0:T(1024)}, u32[]{:S(2)}) copy-start(f32[1024]{0:T(1024)} %param.11) | copy-start | bytes 12292
  44.1 163.9 %all-reduce.4.cloned.1.call-start = ((), (), s32[]{:S(2)}) async-start(), calls=%async_computation.3 | async-start | bytes 131072 | tf_op jit(solution)/shard_map/psum | solution.py:104
  44.8 26.6 %collective-permute-start = (bf16[2,512]{1,0:T(2,128)(2,1)S(1)}, bf16[2,512]{1,0:T(2,128)(2,1)S(1)}, u32[]{:S(2)}, u32[]{:S(2)}) collective-permute-start(bf16[2,512]{1,0:T(2,128)(2,1)S(1)} %get-tuple-element.18), channel_id=1, source_target_pairs={{0,1},{1,2},{2,3},{3,4},{4,5},{5,6},{6,7},{8,9},{9,10},{10,11},{11... | collective-permute-start | bytes 6152 | tf_op jit(solution)/shard_map/ppermute | solution.py:17
  68.5 4.3 %collective-permute-start.1 = (bf16[2,512]{1,0:T(2,128)(2,1)S(1)}, bf16[2,512]{1,0:T(2,128)(2,1)S(1)}, u32[]{:S(2)}, u32[]{:S(2)}) collective-permute-start(bf16[2,512]{1,0:T(2,128)(2,1)S(1)} %get-tuple-element.19), channel_id=1, source_target_pairs={{1,0},{2,1},{3,2},{4,3},{5,4},{6,5},{7,6},{9,8},{10,9},{11,10},{12... | collective-permute-start | bytes 6152 | tf_op jit(solution)/shard_map/ppermute | solution.py:19
  155.6 53.9 %all-to-all-start = ((f32[8,16,1024]{2,1,0:T(8,128)}), f32[8,16,1024]{2,1,0:T(8,128)S(1)}, u32[]{:S(2)}, u32[]{:S(2)}) async-start(f32[8,16,1024]{2,1,0:T(8,128)} %fusion.36), calls=%async_computation.1 | async-start | bytes 1048576 | tf_op jit(solution)/shard_map/all_to_all | solution.py:108
Sparse Core Ops, SparseCore 0:
  44.2 91.2 reduce-scatter.1
  151.3 56.6 all-reduce.3
